TPU v7x, 32 devices: a whole 2x2x4 slice. The times are simulated.
32 devices in a mesh: row: 8 (over z, core), col: 4 (over y, x).
Axes of the slice: x: 2, y: 2, z: 4, core: 2. Of those that a mesh axis runs over, the one named last changes fastest.
Arguments:
- factor: bfloat16 [8192, 8192], P('row', 'col'), as said below
- sel_tiles: int32 [32], replicated, may hold values from 0 to 63, as said below
- coupling: bfloat16 [8192, 2048], P('col', 'row')
Outputs:
- root_inverse: float32 [8192, 8192], P('row', 'col')
- child_inverse: float32 [2048, 8192], P('col', 'row')
Inputs may be any that keep to these rules, and one draw needn't show every extreme that they name: sel_tiles holds 32 distinct tile indices in increasing order; rows of coupling outside the listed tiles are zero. factor is lower triangular with a diagonal between 1 and 1.5.
All inputs are finite; a program needn't handle non-finite values.
Results may differ from a plain program's by a relative error of at most 0.003.
Values may be sent and summed in bfloat16 or wider, within the bound.
A program may use at most 128 MiB of HBM per device.

v0:
```python
import jax
import jax.numpy as jnp
from jax import lax
from jax.sharding import PartitionSpec as P

TILE = 128


def from_root(value, axis, source):
    kept = jnp.where(lax.axis_index(axis) == source, value, 0).astype(value.dtype)
    return lax.psum(kept, axis)


def body(factor, sel_tiles, coupling):
    rows_here = factor.shape[0]
    row_index = lax.axis_index("row")
    whole = lax.all_gather(factor, "row", axis=0, tiled=True)
    ratio = lax.axis_size("row") // lax.axis_size("col")
    offset = row_index % ratio * rows_here
    piece = lax.dynamic_slice_in_dim(whole, offset, rows_here, 1)
    partner = from_root(piece, "col", row_index // ratio)
    gram = lax.dot_general(
        partner, whole, (((0,), (0,)), ((), ())), preferred_element_type=jnp.float32
    )
    coupling_full = lax.all_gather(coupling, "row", axis=1, tiled=True)
    rounded = gram.astype(jnp.bfloat16)
    global_rows = row_index * rows_here + jnp.arange(rows_here, dtype=jnp.int32)
    member = jnp.any((global_rows // TILE)[:, None] == sel_tiles[None, :], axis=1)
    summed = lax.psum_scatter(
        lax.dot_general(
            coupling_full, rounded, (((0,), (1,)), ((), ())), preferred_element_type=jnp.float32
        ),
        "col",
        scatter_dimension=0,
        tiled=True,
    )
    child = jnp.where(member[None, :], -summed, jnp.float32(0.0))
    return (gram, child)


def solution(mesh):
    placed = (P("row", "col"), P(), P("col", "row"))
    return jax.shard_map(
        body,
        mesh=mesh,
        in_specs=placed,
        out_specs=(P("row", "col"), P("col", "row")),
        check_vma=False,
    )
```

profile of v0, /device:TPU:0, one launch (start us, length us, event | category | flops | bytes accessed | tf_op | source)
XLA Modules:
  0.0 817.3 jit_solution(11417977400386051904)
XLA Ops:
  7.2 0.0 all-gather.3.cloned.1.call-start
  7.2 0.7 all-gather.3.cloned.1.call-update
  7.9 0.0 all-reduce.2.cloned.1.call-start
  8.0 293.0 %all-gather.3.cloned.1.call-done = bf16[8192,2048]{1,0:T(8,128)(2,1)} async-done(((bf16[1024,2048]{1,0:T(8,128)(2,1)}), bf16[8192,2048]{1,0:T(8,128)(2,1)}) %all-gather.3.cloned.1.call-update) | async-done | bytes 33554448 | tf_op jit(solution)/shard_map/all_gather | solution.py:17
  300.9 15.0 %dynamic-slice_select_fusion = bf16[8192,1024]{1,0:T(8,128)(2,1)} fusion(bf16[8192,2048]{1,0:T(8,128)(2,1)} %all-gather.3.cloned.1.call-done, s32[]{:T(128)S(6)} %select_n.38, pred[]{:T(512)S(6)} %eq.18), kind=kLoop, calls=%fused_computation | loop fusion | flops 8388608 | bytes 33554436 | tf_op jit(solution)/shard_map/jit(_where)/select_n | solution.py:10
  316.0 0.0 all-reduce.2.cloned.1.call-update
  316.0 0.0 all-gather.5.cloned.1.call-start
  316.0 0.7 all-gather.5.cloned.1.call-update
  316.7 0.0 reduce-scatter.2.cloned.1.call-start
  316.8 304.9 %all-reduce.2.cloned.1.call-done = bf16[8192,1024]{1,0:T(8,128)(2,1)} async-done(((bf16[8192,1024]{1,0:T(8,128)(2,1)}), bf16[8192,1024]{1,0:T(8,128)(2,1)}) %all-reduce.2.cloned.1.call-update) | async-done | bytes 16777232 | tf_op jit(solution)/shard_map/psum | solution.py:11
  621.7 43.9 %fusion.4 = f32[1024,2048]{1,0:T(8,128)} fusion(bf16[8192,1024]{1,0:T(8,128)(2,1)} %all-reduce.2.cloned.1.call-done, bf16[8192,2048]{1,0:T(8,128)(2,1)} %all-gather.3.cloned.1.call-done), kind=kOutput, calls=%fused_computation.14 | convolution fusion | flops 34359738368 | bytes 58720256 | tf_op jit(solution)/shard_map/dot_general | solution.py:22
  665.6 41.2 %all-gather.5.cloned.1.call-done = bf16[2048,2048]{1,0:T(8,128)(2,1)} async-done(((bf16[2048,256]{1,0:T(8,128)(2,1)}), bf16[2048,2048]{1,0:T(8,128)(2,1)}) %all-gather.5.cloned.1.call-update) | async-done | bytes 8388624 | tf_op jit(solution)/shard_map/all_gather | solution.py:25
  706.8 15.6 %convolution_bitcast_fusion = f32[2048,1024]{0,1:T(8,128)} fusion(bf16[2048,2048]{1,0:T(8,128)(2,1)} %all-gather.5.cloned.1.call-done, f32[1024,2048]{1,0:T(8,128)} %fusion.4), kind=kOutput, calls=%fused_computation.1 | convolution fusion | flops 8592031744 | bytes 25165824 | tf_op jit(solution)/shard_map/dot_general | solution.py:30
  722.4 0.0 copy-start
  722.4 0.0 reduce-scatter.2.cloned.1.call-update
  722.5 0.6 copy-done
  723.1 0.1 compare_reduce_fusion
  723.2 83.9 %reduce-scatter.2.cloned.1.call-done = f32[512,1024]{0,1:T(8,128)} async-done(((f32[2048,1024]{0,1:T(8,128)}), f32[512,1024]{0,1:T(8,128)}) %reduce-scatter.2.cloned.1.call-update) | async-done | bytes 2097168 | tf_op jit(solution)/shard_map/reduce_scatter | solution.py:29
  807.1 1.9 negate_select_fusion
  809.0 1.8 copy.6
  (1 shorter events, 0.0 us)
Async XLA Ops:
  7.2 293.8 %all-gather.3.cloned.1.call-start = ((), (), s32[]{:S(2)}) async-start(), calls=%async_computation.1 | async-start | bytes 37748736 | tf_op jit(solution)/shard_map/all_gather | solution.py:17
  7.9 613.8 %all-reduce.2.cloned.1.call-start = ((), (), s32[]{:S(2)}) async-start(), calls=%async_computation.2 | async-start | bytes 33554432 | tf_op jit(solution)/shard_map/psum | solution.py:11
  316.0 390.8 %all-gather.5.cloned.1.call-start = ((), (), s32[]{:S(2)}) async-start(), calls=%async_computation.3 | async-start | bytes 9437184 | tf_op jit(solution)/shard_map/all_gather | solution.py:25
  316.7 490.4 %reduce-scatter.2.cloned.1.call-start = ((), (), s32[]{:S(2)}) async-start(), calls=%async_computation.4 | async-start | bytes 10485760 | tf_op jit(solution)/shard_map/reduce_scatter | solution.py:29
  722.4 0.7 copy-start
Sparse Core Ops, SparseCore 0:
  9.6 291.3 all-gather.2
  316.1 305.5 all-reduce.1
  623.3 83.5 all-gather.4
  722.6 84.4 reduce-scatter.1
where the time goes:
time: 818 us; the launch traced here: 817 us
  waiting for transfers between devices  724 us (89%)
  matrix products  59.6 us (7%)
  other arithmetic  17 us (2%)
  between operations  13.8 us (2%)
    psum x1, waiting for transfers between devices, from_root(): return lax.psum(kept, axis)  305 us
    all_gather x1, waiting for transfers between devices, body(): whole = lax.all_gather(factor, 'row', axis=0, tiled=True)  293 us
    reduce_scatter x1, waiting for transfers between devices, body(): lax.psum_scatter(lax.dot_general(coupling_full, rounded, (((0,), (1,)), (...  83.9 us
    dot_general x1, matrix products, body(): lax.dot_general(partner, whole, (((0,), (0,)), ((), ())), preferred_eleme...  43.9 us
    all_gather x1, waiting for transfers between devices, body(): coupling_full = lax.all_gather(coupling, 'row', axis=1, tiled=True)  41.2 us
  transfers between devices with their start and end apart: 4, of which 4 were waited for; matrix products, arithmetic and copies ran while one was open for 5% of the time, Pallas kernels for 0%

commit v1 on v0

--- a/solution.py
+++ b/solution.py
@@ -22,7 +22,12 @@
     gram = lax.dot_general(
         partner, whole, (((0,), (0,)), ((), ())), preferred_element_type=jnp.float32
     )
-    coupling_full = lax.all_gather(coupling, "row", axis=1, tiled=True)
+    ring = [coupling]
+    for hop in range(7):
+        ring.append(lax.ppermute(ring[-1], "row", [(dev, (dev + 1) % 8) for dev in range(8)]))
+    coupling_full = jnp.roll(
+        jnp.concatenate(ring[::-1], axis=1), (lax.axis_index("row") + 1) * ring[0].shape[1], axis=1
+    )
     rounded = gram.astype(jnp.bfloat16)
     global_rows = row_index * rows_here + jnp.arange(rows_here, dtype=jnp.int32)
     member = jnp.any((global_rows // TILE)[:, None] == sel_tiles[None, :], axis=1)

time: 818 us -> 780 us (0.954)
  waiting for transfers between devices: 724 us -> 656 us
  local copies, waits for them, and re-layouts: 2.42 us -> 33.7 us
    psum x1, waiting for transfers between devices: 305 us -> 163 us  [from_root(): return lax.psum(kept, axis)]
    ppermute x0 -> x7, waiting for transfers between devices: none -> 112 us  [body(): lax.ppermute(ring[-1], 'row', [(dev, (dev + 1) % 8) for dev in range(8)])]
    all_gather x1 -> x0, waiting for transfers between devices: 41.2 us -> none  [body(): coupling_full = lax.all_gather(coupling, 'row', axis=1, tiled=True)]
    unnamed x3 -> x33, local copies, waits for them, and re-layouts: 2.42 us -> 32.6 us
  transfers between devices with their start and end apart: 4 -> 10, of which waited for: 4 -> 10; matrix products, arithmetic and copies ran while one was open for 5% -> 3% of each run, Pallas kernels for 0% -> 0%
where the time goes in v1:
time: 780 us; the launch traced here: 779 us
  waiting for transfers between devices  656 us (84%)
  matrix products  56.5 us (7%)
  local copies, waits for them, and re-layouts  33.7 us (4%)
  other arithmetic  18.5 us (2%)
  between operations  13.8 us (2%)
    all_gather x1, waiting for transfers between devices, body(): whole = lax.all_gather(factor, 'row', axis=0, tiled=True)  293 us
    psum x1, waiting for transfers between devices, from_root(): return lax.psum(kept, axis)  163 us
    ppermute x7, waiting for transfers between devices, body(): lax.ppermute(ring[-1], 'row', [(dev, (dev + 1) % 8) for dev in range(8)])  112 us
    reduce_scatter x1, waiting for transfers between devices, body(): lax.psum_scatter(lax.dot_general(coupling_full, rounded, (((0,), (1,)), (...  87.4 us
    dot_general x1, matrix products, body(): lax.dot_general(partner, whole, (((0,), (0,)), ((), ())), preferred_eleme...  43.1 us
    unnamed x33, local copies, waits for them, and re-layouts  32.6 us
  transfers between devices with their start and end apart: 10, of which 10 were waited for; matrix products, arithmetic and copies ran while one was open for 3% of the time, Pallas kernels for 0%

profile of v1, /device:TPU:0, one launch (start us, length us, event | category | flops | bytes accessed | tf_op | source)
XLA Modules:
  0.0 779.0 jit_solution(4246084666884449865)
XLA Ops:
  7.2 0.0 all-gather.2.cloned.1.call-start
  7.2 0.7 all-gather.2.cloned.1.call-update
  7.9 0.0 all-reduce.2.cloned.1.call-start
  8.0 293.0 %all-gather.2.cloned.1.call-done = bf16[8192,2048]{1,0:T(8,128)(2,1)} async-done(((bf16[1024,2048]{1,0:T(8,128)(2,1)}), bf16[8192,2048]{1,0:T(8,128)(2,1)}) %all-gather.2.cloned.1.call-update) | async-done | bytes 33554448 | tf_op jit(solution)/shard_map/all_gather | solution.py:17
  300.9 15.0 %dynamic-slice_select_fusion = bf16[8192,1024]{1,0:T(8,128)(2,1)} fusion(bf16[8192,2048]{1,0:T(8,128)(2,1)} %all-gather.2.cloned.1.call-done, s32[]{:T(128)S(6)} %select_n.50, pred[]{:T(512)S(6)} %eq.21), kind=kLoop, calls=%fused_computation | loop fusion | flops 8388608 | bytes 33554436 | tf_op jit(solution)/shard_map/jit(_where)/select_n | solution.py:10
  316.0 0.0 all-reduce.2.cloned.1.call-update
  316.0 0.0 reduce-scatter.2.cloned.1.call-start
  316.0 1.1 copy-done
  317.2 0.2 collective-permute-start
  317.4 15.8 %collective-permute-done = bf16[2048,256]{1,0:T(8,128)(2,1)S(1)} collective-permute-done((bf16[2048,256]{1,0:T(8,128)(2,1)S(1)}, bf16[2048,256]{1,0:T(8,128)(2,1)S(1)}, u32[]{:S(2)}, u32[]{:S(2)}) %collective-permute-start) | collective-permute-done | bytes 1048608 | tf_op jit(solution)/shard_map/ppermute | solution.py:27
  333.2 0.0 collective-permute-start.1
  333.2 16.0 %collective-permute-done.1 = bf16[2048,256]{1,0:T(8,128)(2,1)S(1)} collective-permute-done((bf16[2048,256]{1,0:T(8,128)(2,1)S(1)}, bf16[2048,256]{1,0:T(8,128)(2,1)S(1)}, u32[]{:S(2)}, u32[]{:S(2)}) %collective-permute-start.1) | collective-permute-done | bytes 1048608 | tf_op jit(solution)/shard_map/ppermute | solution.py:27
  349.2 16.0 %collective-permute-done.2 = bf16[2048,256]{1,0:T(8,128)(2,1)S(1)} collective-permute-done((bf16[2048,256]{1,0:T(8,128)(2,1)S(1)}, bf16[2048,256]{1,0:T(8,128)(2,1)S(1)}, u32[]{:S(2)}, u32[]{:S(2)}) %collective-permute-start.2) | collective-permute-done | bytes 1048608 | tf_op jit(solution)/shard_map/ppermute | solution.py:27
  365.3 1.0 copy-done.1
  366.2 0.0 collective-permute-start.3
  366.2 16.0 %collective-permute-done.3 = bf16[2048,256]{1,0:T(8,128)(2,1)S(1)} collective-permute-done((bf16[2048,256]{1,0:T(8,128)(2,1)S(1)}, bf16[2048,256]{1,0:T(8,128)(2,1)S(1)}, u32[]{:S(2)}, u32[]{:S(2)}) %collective-permute-start.3) | collective-permute-done | bytes 1048608 | tf_op jit(solution)/shard_map/ppermute | solution.py:27
  382.3 1.0 copy-done.3
  383.2 0.0 collective-permute-start.4
  383.2 16.0 %collective-permute-done.4 = bf16[2048,256]{1,0:T(8,128)(2,1)S(1)} collective-permute-done((bf16[2048,256]{1,0:T(8,128)(2,1)S(1)}, bf16[2048,256]{1,0:T(8,128)(2,1)S(1)}, u32[]{:S(2)}, u32[]{:S(2)}) %collective-permute-start.4) | collective-permute-done | bytes 1048608 | tf_op jit(solution)/shard_map/ppermute | solution.py:27
  399.3 1.0 copy-done.5
  400.2 0.0 collective-permute-start.5
  400.2 16.1 %collective-permute-done.5 = bf16[2048,256]{1,0:T(8,128)(2,1)} collective-permute-done((bf16[2048,256]{1,0:T(8,128)(2,1)S(1)}, bf16[2048,256]{1,0:T(8,128)(2,1)}, u32[]{:S(2)}, u32[]{:S(2)}) %collective-permute-start.5) | collective-permute-done | bytes 1048608 | tf_op jit(solution)/shard_map/ppermute | solution.py:27
  416.4 16.3 %collective-permute-done.6 = bf16[2048,256]{1,0:T(8,128)(2,1)} collective-permute-done((bf16[2048,256]{1,0:T(8,128)(2,1)}, bf16[2048,256]{1,0:T(8,128)(2,1)}, u32[]{:S(2)}, u32[]{:S(2)}) %collective-permute-start.6) | collective-permute-done | bytes 1048608 | tf_op jit(solution)/shard_map/ppermute | solution.py:27
  432.7 2.3 constant_dynamic-update-slice_fusion.15
  435.0 2.3 constant_dynamic-update-slice_fusion.14
  437.3 2.4 constant_dynamic-update-slice_fusion.13
  439.8 2.4 constant_dynamic-update-slice_fusion.12
  442.1 2.4 constant_dynamic-update-slice_fusion.11
  444.5 1.1 constant_dynamic-update-slice_fusion.10
  445.6 1.1 constant_dynamic-update-slice_fusion.9
  446.7 1.1 constant_dynamic-update-slice_fusion.8
  447.8 2.3 constant_dynamic-update-slice_fusion.7
  450.1 2.3 constant_dynamic-update-slice_fusion.6
  452.4 1.1 constant_dynamic-update-slice_fusion.5
  453.5 1.1 constant_dynamic-update-slice_fusion.4
  454.5 1.1 constant_dynamic-update-slice_fusion.3
  455.6 1.1 constant_dynamic-update-slice_fusion.2
  456.7 1.1 constant_dynamic-update-slice_fusion.1
  457.9 1.1 constant_dynamic-update-slice_fusion
  458.9 162.8 %all-reduce.2.cloned.1.call-done = bf16[8192,1024]{1,0:T(8,128)(2,1)} async-done(((bf16[8192,1024]{1,0:T(8,128)(2,1)}), bf16[8192,1024]{1,0:T(8,128)(2,1)}) %all-reduce.2.cloned.1.call-update) | async-done | bytes 16777232 | tf_op jit(solution)/shard_map/psum | solution.py:11
  621.7 43.1 %fusion.7 = f32[1024,2048]{1,0:T(8,128)S(1)} fusion(bf16[8192,1024]{1,0:T(8,128)(2,1)} %all-reduce.2.cloned.1.call-done, bf16[8192,2048]{1,0:T(8,128)(2,1)} %all-gather.2.cloned.1.call-done), kind=kOutput, calls=%fused_computation.32 | convolution fusion | flops 34359738368 | bytes 58720256 | tf_op jit(solution)/shard_map/dot_general | solution.py:22
  664.8 0.0 copy-start.8
  664.8 3.4 copy-done.8
  668.2 13.4 %fusion = f32[2048,1024]{1,0:T(8,128)} fusion(bf16[2048,4096]{1,0:T(8,128)(2,1)} %constant_dynamic-update-slice_fusion, s32[]{:T(128)S(6)} %select_n.54, f32[1024,2048]{1,0:T(8,128)S(1)} %fusion.7), kind=kOutput, calls=%fused_computation.1 | convolution fusion | flops 8592031744 | bytes 25165828 | tf_op jit(solution)/shard_map/dot_general | solution.py:35
  681.6 0.0 reduce-scatter.2.cloned.1.call-update
  681.7 0.1 compare_reduce_fusion
  681.8 87.4 %reduce-scatter.2.cloned.1.call-done = f32[512,1024]{1,0:T(8,128)} async-done(((f32[2048,1024]{1,0:T(8,128)}), f32[512,1024]{1,0:T(8,128)}) %reduce-scatter.2.cloned.1.call-update) | async-done | bytes 2097168 | tf_op jit(solution)/shard_map/reduce_scatter | solution.py:34
  769.1 3.3 negate_select_fusion
  (15 shorter events, 0.0 us)
Async XLA Ops:
  7.2 293.8 %all-gather.2.cloned.1.call-start = ((), (), s32[]{:S(2)}) async-start(), calls=%async_computation.1 | async-start | bytes 37748736 | tf_op jit(solution)/shard_map/all_gather | solution.py:17
  7.9 613.8 %all-reduce.2.cloned.1.call-start = ((), (), s32[]{:S(2)}) async-start(), calls=%async_computation.2 | async-start | bytes 33554432 | tf_op jit(solution)/shard_map/psum | solution.py:11
  316.0 1.2 copy-start
  316.0 453.1 %reduce-scatter.2.cloned.1.call-start = ((), (), s32[]{:S(2)}) async-start(), calls=%async_computation.3 | async-start | bytes 10485760 | tf_op jit(solution)/shard_map/reduce_scatter | solution.py:34
  317.2 16.0 %collective-permute-start = (bf16[2048,256]{1,0:T(8,128)(2,1)S(1)}, bf16[2048,256]{1,0:T(8,128)(2,1)S(1)}, u32[]{:S(2)}, u32[]{:S(2)}) collective-permute-start(bf16[2048,256]{1,0:T(8,128)(2,1)S(1)} %copy-done), channel_id=1, source_target_pairs={{0,4},{4,8},{8,12},{12,16},{16,20},{20,24},{24,28},{28,0},{1,5},{5... | collective-permute-start | bytes 3145736 | tf_op jit(solution)/shard_map/ppermute | solution.py:27
  333.2 16.0 %collective-permute-start.1 = (bf16[2048,256]{1,0:T(8,128)(2,1)S(1)}, bf16[2048,256]{1,0:T(8,128)(2,1)S(1)}, u32[]{:S(2)}, u32[]{:S(2)}) collective-permute-start(bf16[2048,256]{1,0:T(8,128)(2,1)S(1)} %collective-permute-done), channel_id=1, source_target_pairs={{0,4},{4,8},{8,12},{12,16},{16,20},{20,24},{24,28},{28,0},{1,5},{5... | collective-permute-start | bytes 3145736 | tf_op jit(solution)/shard_map/ppermute | solution.py:27
  349.2 16.0 %collective-permute-start.2 = (bf16[2048,256]{1,0:T(8,128)(2,1)S(1)}, bf16[2048,256]{1,0:T(8,128)(2,1)S(1)}, u32[]{:S(2)}, u32[]{:S(2)}) collective-permute-start(bf16[2048,256]{1,0:T(8,128)(2,1)S(1)} %collective-permute-done.1), channel_id=1, source_target_pairs={{0,4},{4,8},{8,12},{12,16},{16,20},{20,24},{24,28},{28,0},{1,5},{5... | collective-permute-start | bytes 3145736 | tf_op jit(solution)/shard_map/ppermute | solution.py:27
  365.3 1.0 copy-start.1
  366.2 16.0 %collective-permute-start.3 = (bf16[2048,256]{1,0:T(8,128)(2,1)S(1)}, bf16[2048,256]{1,0:T(8,128)(2,1)S(1)}, u32[]{:S(2)}, u32[]{:S(2)}) collective-permute-start(bf16[2048,256]{1,0:T(8,128)(2,1)S(1)} %collective-permute-done.2), channel_id=1, source_target_pairs={{0,4},{4,8},{8,12},{12,16},{16,20},{20,24},{24,28},{28,0},{1,5},{5... | collective-permute-start | bytes 3145736 | tf_op jit(solution)/shard_map/ppermute | solution.py:27
  382.3 1.0 copy-start.3
  383.2 16.0 %collective-permute-start.4 = (bf16[2048,256]{1,0:T(8,128)(2,1)S(1)}, bf16[2048,256]{1,0:T(8,128)(2,1)S(1)}, u32[]{:S(2)}, u32[]{:S(2)}) collective-permute-start(bf16[2048,256]{1,0:T(8,128)(2,1)S(1)} %collective-permute-done.3), channel_id=1, source_target_pairs={{0,4},{4,8},{8,12},{12,16},{16,20},{20,24},{24,28},{28,0},{1,5},{5... | collective-permute-start | bytes 3145736 | tf_op jit(solution)/shard_map/ppermute | solution.py:27
  399.3 1.0 copy-start.5
  400.2 16.1 %collective-permute-start.5 = (bf16[2048,256]{1,0:T(8,128)(2,1)S(1)}, bf16[2048,256]{1,0:T(8,128)(2,1)}, u32[]{:S(2)}, u32[]{:S(2)}) collective-permute-start(bf16[2048,256]{1,0:T(8,128)(2,1)S(1)} %collective-permute-done.4), channel_id=1, source_target_pairs={{0,4},{4,8},{8,12},{12,16},{16,20},{20,24},{24,28},{28,0},{1,5},{5... | collective-permute-start | bytes 3145736 | tf_op jit(solution)/shard_map/ppermute | solution.py:27
  416.4 16.3 %collective-permute-start.6 = (bf16[2048,256]{1,0:T(8,128)(2,1)}, bf16[2048,256]{1,0:T(8,128)(2,1)}, u32[]{:S(2)}, u32[]{:S(2)}) collective-permute-start(bf16[2048,256]{1,0:T(8,128)(2,1)} %collective-permute-done.5), channel_id=1, source_target_pairs={{0,4},{4,8},{8,12},{12,16},{16,20},{20,24},{24,28},{28,0},{1,5},{5... | collective-permute-start | bytes 3145736 | tf_op jit(solution)/shard_map/ppermute | solution.py:27
  416.4 36.0 %copy-start.6 = (bf16[2048,256]{1,0:T(8,128)(2,1)S(1)}, bf16[2048,256]{1,0:T(8,128)(2,1)}, u32[]{:S(2)}) copy-start(bf16[2048,256]{1,0:T(8,128)(2,1)} %copy-done.5) | copy-start | bytes 3145732
  416.4 37.1 %copy-start.4 = (bf16[2048,256]{1,0:T(8,128)(2,1)S(1)}, bf16[2048,256]{1,0:T(8,128)(2,1)}, u32[]{:S(2)}) copy-start(bf16[2048,256]{1,0:T(8,128)(2,1)} %copy-done.3) | copy-start | bytes 3145732
  416.4 38.2 %copy-start.2 = (bf16[2048,256]{1,0:T(8,128)(2,1)S(1)}, bf16[2048,256]{1,0:T(8,128)(2,1)}, u32[]{:S(2)}) copy-start(bf16[2048,256]{1,0:T(8,128)(2,1)} %copy-done.1) | copy-start | bytes 3145732
  664.8 3.4 copy-start.8
  668.2 13.5 %copy-start.7 = (s32[32]{0:T(128)S(1)}, s32[32]{0:T(128)}, u32[]{:S(2)}) copy-start(s32[32]{0:T(128)} %param.4) | copy-start | bytes 388
Sparse Core Ops, SparseCore 0:
  9.6 291.3 all-gather.1
  316.1 305.5 all-reduce.1
  681.8 87.3 reduce-scatter.1
